TPU v7x, 512 devices: a whole 4x8x8 slice. The times are simulated.
512 devices in a mesh: dp: 32 (over y_hi, x, core), mp: 16 (over y_lo, z).
Axes of the slice: x: 4, y: 8 (y_hi: 4, y_lo: 2; y = y_hi * 2 + y_lo), z: 8, core: 2. Of those that a mesh axis runs over, the one named last changes fastest.
Arguments:
- activations: bfloat16 [32, 128, 4096], P('dp', None, 'mp'), may hold values from -6 to 6
- gradients: bfloat16 [32, 128, 11008], P('dp', None, 'mp'), may hold values from -12 to 12, as said below
- basis_in: bfloat16 [4096, 4096], P(None, 'mp'), may hold values from -0.09375 to 0.09375
- basis_out: bfloat16 [11008, 11008], P('mp', 'dp'), may hold values from -0.0546875 to 0.0546875
Outputs:
- eigen_diag: float32 [11008, 4096], P('dp', 'mp')
Inputs may be any that keep to these rules, and one draw needn't show every extreme that they name: `gradients`: gradients are real-valued with varying scales.
All inputs are finite; a program needn't handle non-finite values.
Results may differ from a plain program's by a relative error of at most 0.02.
Values may be sent and summed in bfloat16 or wider, within the bound.
A program may use at most 64 MiB of HBM per device.

v0:
```python
import jax
import jax.numpy as jnp
from jax import lax
from jax.sharding import PartitionSpec as P


def sent_to_all(shard, axis):
    count = lax.axis_size(axis)
    return lax.all_to_all(
        jnp.broadcast_to(shard[None], (count, *shard.shape)), axis, 0, 0, tiled=True
    )


def joined_along(tiles, dim):
    dims = list(tiles.shape[1:])
    dims[dim] *= tiles.shape[0]
    return jnp.moveaxis(tiles, 0, dim).reshape(dims)


def collect(shard, axis, dim):
    tiles = sent_to_all(shard, axis)
    return joined_along(tiles, dim)


def shards(activations, gradients, basis_in, basis_out):
    gathered = lax.all_gather(gradients, "dp", axis=0, tiled=True)
    seq_count = gathered.shape[0]
    seq_tokens = gathered.shape[1]
    flat_rows = gathered.reshape(seq_count * seq_tokens, gathered.shape[2])
    out_width = basis_out.shape[1]
    partial_sum = jnp.dot(flat_rows, basis_out, preferred_element_type=jnp.float32)
    proj_grad = lax.psum(partial_sum.astype(jnp.bfloat16), "mp")
    proj_grad = proj_grad.reshape(seq_count, seq_tokens, out_width)
    whole_acts = collect(activations, "mp", 2)
    local_tokens = whole_acts.shape[0] * whole_acts.shape[1]
    act_rows = whole_acts.reshape(local_tokens, whole_acts.shape[2])
    proj_act = jnp.dot(act_rows, basis_in, preferred_element_type=jnp.float32).astype(jnp.bfloat16)
    proj_act = proj_act.reshape(whole_acts.shape[0], whole_acts.shape[1], basis_in.shape[1])
    every_act = collect(proj_act, "dp", 0)
    seq_grad = jnp.einsum("sti,stj->sij", proj_grad, every_act, preferred_element_type=jnp.float32)
    squares = jnp.sum(seq_grad * seq_grad, axis=0)
    return squares * (1.0 / (seq_count * seq_tokens))


def solution(mesh):
    return jax.shard_map(
        shards,
        mesh=mesh,
        in_specs=(P("dp", None, "mp"), P("dp", None, "mp"), P(None, "mp"), P("mp", "dp")),
        out_specs=P("dp", "mp"),
        check_vma=False,
    )
```

profile of v0, /device:TPU:2, one launch (start us, length us, event | category | flops | bytes accessed | tf_op | source)
XLA Modules:
  0.0 298.8 jit_solution(9737288411021023752)
XLA Ops:
  6.5 0.0 copy-start
  6.5 0.0 all-gather.2.cloned.1.call-start
  6.5 0.7 all-gather.2.cloned.1.call-update
  7.3 0.9 copy.11
  8.2 0.2 broadcast_in_dim.14
  8.4 37.5 %all_to_all.10 = bf16[16,1,128,256]{2,3,1,0:T(8,128)(2,1)S(1)} all-to-all(bf16[16,1,128,256]{2,3,1,0:T(8,128)(2,1)S(1)} %broadcast_in_dim.14), channel_id=1, replica_groups=mesh['dp'=32,'mp'=16] {'mp'}, dimensions={0} | all-to-all | bytes 2097152 | tf_op jit(solution)/shard_map/all_to_all | solution.py:9
  46.0 0.0 copy-done
  46.0 0.6 convolution_convert_fusion
  46.5 0.0 copy-start.1
  46.6 1.6 broadcast_in_dim.15
  48.2 9.5 %all-to-all-start.1 = ((bf16[32,1,128,256]{3,2,1,0:T(8,128)(2,1)}), bf16[32,1,128,256]{3,2,1,0:T(8,128)(2,1)}, u32[]{:S(2)}, u32[]{:S(2)}) async-start(bf16[32,1,128,256]{3,2,1,0:T(8,128)(2,1)} %broadcast_in_dim.15), calls=%async_computation.1 | async-start | bytes 4194304 | tf_op jit(solution)/shard_map/all_to_all | solution.py:9
  57.7 0.0 all-reduce.2.cloned.1.call-start
  57.8 57.5 %all-gather.2.cloned.1.call-done = bf16[32,128,688]{1,2,0:T(8,128)(2,1)} async-done(((bf16[1,128,688]{1,2,0:T(8,128)(2,1)}), bf16[32,128,688]{1,2,0:T(8,128)(2,1)}) %all-gather.2.cloned.1.call-update) | async-done | bytes 5636112 | tf_op jit(solution)/shard_map/all_gather | solution.py:26
  115.3 0.0 copy-done.1
  115.3 5.0 %fusion.7 = bf16[43,32,8,128]{3,2,1,0:T(8,128)(2,1)S(1)} fusion(bf16[688,344]{1,0:T(8,128)(2,1)S(1)} %copy-done.1, bf16[32,128,688]{1,2,0:T(8,128)(2,1)} %all-gather.2.cloned.1.call-done), kind=kOutput, calls=%fused_computation.7 | convolution fusion | flops 1940226048 | bytes 8927488 | tf_op jit(solution)/shard_map/dot_general | solution.py:31
  120.3 2.1 copy.24
  122.4 0.0 all-reduce.2.cloned.1.call-update
  122.4 9.0 %all-to-all-done.1 = bf16[32,1,128,256]{3,2,1,0:T(8,128)(2,1)} async-done(((bf16[32,1,128,256]{3,2,1,0:T(8,128)(2,1)}), bf16[32,1,128,256]{3,2,1,0:T(8,128)(2,1)}, u32[]{:S(2)}, u32[]{:S(2)}) %all-to-all-start.1) | async-done | bytes 2097184 | tf_op jit(solution)/shard_map/all_to_all | solution.py:9
  131.3 155.8 %all-reduce.2.cloned.1.call-done = bf16[32,128,344]{1,2,0:T(8,128)(2,1)} async-done(((bf16[32,128,344]{1,2,0:T(8,128)(2,1)}), bf16[32,128,344]{1,2,0:T(8,128)(2,1)}) %all-reduce.2.cloned.1.call-update) | async-done | bytes 2818064 | tf_op jit(solution)/shard_map/psum | solution.py:32
  287.1 4.1 %multiply_reduce_fusion = f32[344,256]{1,0:T(8,128)S(1)} fusion(bf16[32,128,344]{1,2,0:T(8,128)(2,1)} %all-reduce.2.cloned.1.call-done, bf16[32,1,128,256]{3,2,1,0:T(8,128)(2,1)} %all-to-all-done.1), kind=kOutput, calls=%fused_computation | convolution fusion | flops 726968320 | bytes 5267456 | tf_op jit(solution)/shard_map/sti,stj->sij/dot_general | solution.py:40
  291.2 0.8 broadcast_multiply_fusion
Async XLA Ops:
  6.5 39.4 %copy-start = (bf16[4096,256]{1,0:T(8,128)(2,1)S(1)}, bf16[4096,256]{1,0:T(8,128)(2,1)}, u32[]{:S(2)}) copy-start(bf16[4096,256]{1,0:T(8,128)(2,1)} %param.6) | copy-start | bytes 6291460
  6.5 108.7 %all-gather.2.cloned.1.call-start = ((), (), s32[]{:S(2)}) async-start(), calls=%async_computation.2 | async-start | bytes 5812224 | tf_op jit(solution)/shard_map/all_gather | solution.py:26
  46.5 68.7 %copy-start.1 = (bf16[688,344]{1,0:T(8,128)(2,1)S(1)}, bf16[688,344]{1,0:T(8,128)(2,1)}, u32[]{:S(2)}) copy-start(bf16[688,344]{1,0:T(8,128)(2,1)} %param.7) | copy-start | bytes 1420036
  48.2 83.1 %all-to-all-start.1 = ((bf16[32,1,128,256]{3,2,1,0:T(8,128)(2,1)}), bf16[32,1,128,256]{3,2,1,0:T(8,128)(2,1)}, u32[]{:S(2)}, u32[]{:S(2)}) async-start(bf16[32,1,128,256]{3,2,1,0:T(8,128)(2,1)} %broadcast_in_dim.15), calls=%async_computation.1 | async-start | bytes 4194304 | tf_op jit(solution)/shard_map/all_to_all | solution.py:9
  57.7 229.4 %all-reduce.2.cloned.1.call-start = ((), (), s32[]{:S(2)}) async-start(), calls=%async_computation.3 | async-start | bytes 5636096 | tf_op jit(solution)/shard_map/psum | solution.py:32
Sparse Core Ops, SparseCore 0:
  10.5 104.6 all-gather.1
  122.5 164.5 all-reduce.1
where the time goes:
time: 299 us
  waiting for transfers between devices  223 us (75%)
  blocking collectives  37.5 us (13%)
  between operations  13.5 us (5%)
  matrix products  9.65 us (3%)
  starting transfers between devices  9.55 us (3%)
  local copies, waits for them, and re-layouts  4.9 us (2%)
    psum x1, waiting for transfers between devices, shards(): proj_grad = lax.psum(partial_sum.astype(jnp.bfloat16), 'mp')  156 us
    all_gather x1, waiting for transfers between devices, shards(): gathered = lax.all_gather(gradients, 'dp', axis=0, tiled=True)  57.5 us
    all_to_all x1, blocking collectives, sent_to_all(): lax.all_to_all(jnp.broadcast_to(shard[None], (count, *shard.shape)), axis...  37.5 us
    all_to_all x1, starting transfers between devices, sent_to_all(): lax.all_to_all(jnp.broadcast_to(shard[None], (count, *shard.shape)), axis...  9.5 us
    all_to_all x1, waiting for transfers between devices, sent_to_all(): lax.all_to_all(jnp.broadcast_to(shard[None], (count, *shard.shape)), axis...  8.96 us
  transfers between devices with their start and end apart: 3, of which 3 were waited for; matrix products, arithmetic and copies ran while one was open for 4% of the time, Pallas kernels for 0%

commit v1 on v0

v1 whole, which is shorter than its diff:
```python
import functools

import jax
import jax.numpy as jnp
from jax import lax
from jax.experimental import pallas as pl
from jax.experimental.pallas import tpu as pltpu
from jax.sharding import PartitionSpec as P

MESH = pl.DeviceIdType.MESH
NX, NYH, NYL, NZ = 4, 4, 2, 8
F32, BF16 = jnp.float32, jnp.bfloat16


def kernel(
    dims, gt_ref, bt_ref, act_ref, bin_hbm, out_ref,
    bt, g, act, binv, paloc, pa, part, rsb, pg, acc, xrecv, ysend, yrecv,
    send_sems, recv_sems,
):
    feat, seq, half, chunk, width = dims
    dp, mp = lax.axis_index("dp"), lax.axis_index("mp")
    core, x, yh = dp % 2, (dp // 2) % NX, dp // (2 * NX)
    yl, z = mp // NZ, mp % NZ

    def dev(yh_=None, x_=None, c_=None, yl_=None, z_=None):
        yh_ = yh if yh_ is None else yh_
        x_ = x if x_ is None else x_
        c_ = core if c_ is None else c_
        yl_ = yl if yl_ is None else yl_
        z_ = z if z_ is None else z_
        return ((yh_ * NX + x_) * 2 + c_, yl_ * NZ + z_)

    sibling = dev(c_=1 - core)
    ypart = dev(yl_=1 - yl)
    xn = {1: dev(x_=(x + 1) % NX), -1: dev(x_=(x + NX - 1) % NX)}
    zn = {1: dev(z_=(z + 1) % NZ), -1: dev(z_=(z + NZ - 1) % NZ)}

    barrier = pltpu.get_barrier_semaphore()
    peers = [sibling, xn[1], xn[-1], zn[1], zn[-1]]
    y = yh * NYL + yl
    for k in range(1, NYH * NYL):
        yy = (y + k) % (NYH * NYL)
        peers.append(dev(yh_=yy // NYL, yl_=yy % NYL))
    for peer in peers:
        pl.semaphore_signal(barrier, inc=1, device_id=peer, device_id_type=MESH)
    pl.semaphore_wait(barrier, len(peers))

    counter = [0]
    sent = []

    def take(n=1):
        base = counter[0]
        counter[0] += n
        return base

    def send(src, dst, ssem, rsem, to):
        copy = pltpu.make_async_remote_copy(
            src_ref=src, dst_ref=dst, send_sem=send_sems.at[ssem], recv_sem=recv_sems.at[rsem],
            device_id=to, device_id_type=MESH,
        )
        copy.start()
        sent.append(copy)

    def arrived(dst, rsem):
        pltpu.make_async_copy(dst, dst, recv_sems.at[rsem]).wait()

    s_bt = take(3)
    s_act0 = take(1)
    s_gy, s_gx = take(4), take(16)
    s_py, s_px = take(4), take(16)
    s_actz = take(16)
    s_rs, s_ag = take(32), take(32)
    s_out = take(2)
    s_loc = take(3)

    hcls, aidx = yh % 2, yh // 2

    def y_start(src, place, sbase):
        for k in (1, 3, 2):
            send(src, place(0, aidx, yl), sbase + k, sbase + aidx * 2 + yl, dev(yh_=(yh + k) % NYH, yl_=hcls))

        def own():
            pltpu.make_async_copy(src, place(0, aidx, yl), recv_sems.at[sbase + aidx * 2 + yl]).start()

        def other():
            pltpu.make_async_remote_copy(
                src_ref=src, dst_ref=place(0, aidx, yl), send_sem=send_sems.at[sbase],
                recv_sem=recv_sems.at[sbase + aidx * 2 + yl], device_id=ypart, device_id_type=MESH,
            ).start()

        pl.when(yl == hcls)(own)
        pl.when(yl != hcls)(other)

    def y_finish(src, place, sbase):
        def other():
            pltpu.make_async_remote_copy(
                src_ref=src, dst_ref=place(0, aidx, yl), send_sem=send_sems.at[sbase],
                recv_sem=recv_sems.at[sbase + aidx * 2 + yl], device_id=ypart, device_id_type=MESH,
            ).wait_send()

        pl.when(yl != hcls)(other)

    def y_to_x(place, sbase, xbase, a, f):
        arrived(place(0, a, f), sbase + a * 2 + f)
        for d, slot in ((1, 1), (-1, 2)):
            send(place(0, a, f), place(slot, a, f), xbase + slot * 4 + a * 2 + f, xbase + slot * 4 + a * 2 + f, xn[d])

    def x_near(place, xbase, a, f):
        for d, slot in ((1, 1), (-1, 2)):
            arrived(place(slot, a, f), xbase + slot * 4 + a * 2 + f)
            if f == slot - 1:
                send(place(slot, a, f), place(3, a, f), xbase + 12 + a * 2 + f, xbase + 12 + a * 2 + f, xn[d])

    def x_far(place, xbase, a, f):
        arrived(place(3, a, f), xbase + 12 + a * 2 + f)

    def g_place(slot, a, f):
        return g.at[slot, f, :, pl.ds(pl.multiple_of(a * seq, 128), seq)]

    def p_place(slot, a, f):
        return pa.at[slot, pl.ds(pl.multiple_of(a * seq, 16), seq), pl.ds(pl.multiple_of(f * width, 128), width)]

    def bt_place(f, c):
        return bt.at[f, pl.ds(pl.multiple_of(c * half, 16), half), :]

    def start():
        pltpu.make_async_copy(bin_hbm, binv, recv_sems.at[s_loc]).start()
        pltpu.make_async_copy(bt_ref, bt_place(yl, core), recv_sems.at[s_loc + 1]).start()
        pltpu.make_async_copy(act_ref, act.at[yl, z], recv_sems.at[s_loc + 2]).start()
        send(act_ref, act.at[yl, z], s_act0, s_act0, ypart)
        y_start(gt_ref, g_place, s_gy)
        send(bt_ref, bt_place(yl, core), s_bt, s_bt, sibling)
        send(bt_ref, bt_place(yl, core), s_bt + 1, s_bt + 1, ypart)

    def bt_forward():
        arrived(bt_place(1 - yl, core), s_bt + 1)
        send(bt_place(1 - yl, core), bt_place(1 - yl, core), s_bt + 2, s_bt + 2, sibling)

    def bt_ready():
        arrived(bt_place(yl, 1 - core), s_bt)
        arrived(bt_place(1 - yl, 1 - core), s_bt + 2)
        arrived(bt_place(yl, core), s_loc + 1)

    def reach(f, d):
        return 4 if (f == 0) == (d == 1) else 3

    def act_sem(f, d, k):
        return s_actz + f * 8 + (0 if d == 1 else 4) + k

    def act_first():
        arrived(act.at[1 - yl, z], s_act0)
        for d in (1, -1):
            send(act_ref, act.at[yl, z], act_sem(yl, d, 0), act_sem(yl, d, 0), zn[d])
            send(act.at[1 - yl, z], act.at[1 - yl, z], act_sem(1 - yl, d, 0), act_sem(1 - yl, d, 0), zn[d])

    def act_step(k):
        for f in range(2):
            for d in (1, -1):
                n = reach(f, d)
                if k <= n:
                    zz = (z + NZ - d * k) % NZ
                    arrived(act.at[f, zz], act_sem(f, d, k - 1))
                    if k < n:
                        send(act.at[f, zz], act.at[f, zz], act_sem(f, d, k), act_sem(f, d, k), zn[d])

    def project_acts():
        arrived(act.at[yl, z], s_loc + 2)
        arrived(binv, s_loc)

        def body(i, total):
            rows = pl.ds(pl.multiple_of(i * width, 128), width)
            return total + jnp.dot(act[i // NZ, i % NZ], binv[rows, :], preferred_element_type=F32)

        total = lax.fori_loop(0, NYL * NZ, body, jnp.zeros((seq, width), F32))
        paloc[...] = total.astype(BF16)

    def project(grp):
        def body(r, carry):
            rows = pl.ds(pl.multiple_of(r * chunk, 16), chunk)
            t = jnp.dot(bt[0, rows, :], g[grp, 0], preferred_element_type=F32)
            t = t + jnp.dot(bt[1, rows, :], g[grp, 1], preferred_element_type=F32)
            t = t.astype(BF16)
            part[grp, r] = t[:, :seq]
            part[grp, r + 4] = t[:, seq:]
            return carry

        lax.fori_loop(0, 4, body, 0)

    def rlen(grp, d):
        return 4 if (grp % 2 == 0) == (d == 1) else 3

    def rs_slot(d, k):
        return (0 if d == 1 else 4) + k

    def rs_step(grp, k):
        for d in (1, -1):
            n = rlen(grp, d)
            if k < n:
                j = (z + NZ + d * (n - k)) % NZ
                if k == 0:
                    src = part.at[grp, j]
                else:
                    slot = rs_slot(d, k - 1)
                    src = rsb.at[grp, slot]
                    arrived(src, s_rs + grp * 8 + slot)
                    rsb[grp, slot] = (rsb[grp, slot].astype(F32) + part[grp, j].astype(F32)).astype(BF16)
                s = s_rs + grp * 8 + rs_slot(d, k)
                send(src, rsb.at[grp, rs_slot(d, k)], s, s, zn[d])

    def pg_place(grp, j):
        return pg.at[grp, pl.ds(pl.multiple_of(j * chunk, 16), chunk), :]

    def ag_sem(grp, d, k):
        return s_ag + grp * 8 + rs_slot(d, k)

    def rs_last(grp):
        total = part[grp, z].astype(F32)
        for d in (1, -1):
            slot = rs_slot(d, rlen(grp, d) - 1)
            arrived(rsb.at[grp, slot], s_rs + grp * 8 + slot)
            total = total + rsb[grp, slot].astype(F32)
        pg[grp, pl.ds(pl.multiple_of(z * chunk, 16), chunk), :] = total.astype(BF16)
        for d in (1, -1):
            send(pg_place(grp, z), pg_place(grp, z), ag_sem(grp, d, 0), ag_sem(grp, d, 0), zn[d])

    def ag_step(grp, k):
        for d in (1, -1):
            n = rlen(grp, d)
            if k <= n:
                j = (z + NZ - d * k) % NZ
                arrived(pg_place(grp, j), ag_sem(grp, d, k - 1))
                if k < n:
                    send(pg_place(grp, j), pg_place(grp, j), ag_sem(grp, d, k), ag_sem(grp, d, k), zn[d])

    def squares(grp, first):
        def body(r, carry):
            rows = pl.ds(pl.multiple_of(r * chunk, 16), chunk)
            total = None if first else acc[rows, :]
            for a in range(2):
                lhs = pg[grp, pl.ds(pl.multiple_of((a * 4 + r) * chunk, 16), chunk), :]
                t = jnp.dot(lhs, pa[grp, a * seq:(a + 1) * seq, :], preferred_element_type=F32)
                total = t * t if total is None else total + t * t
            acc[rows, :] = total
            return carry

        lax.fori_loop(0, 4, body, 0)

    def out_core():
        theirs = acc.at[pl.ds(pl.multiple_of((1 - core) * half, 8), half), :]
        send(theirs, xrecv, s_out, s_out, sibling)
        arrived(xrecv, s_out)

    def out_y():
        mine = pl.ds(pl.multiple_of(core * half, 8), half)
        away = pl.ds(pl.multiple_of((1 - yl) * width, 128), width)
        keep = pl.ds(pl.multiple_of(yl * width, 128), width)
        ysend[...] = (acc[mine, away] + xrecv[:, away]).astype(BF16)
        send(ysend, yrecv, s_out + 1, s_out + 1, ypart)
        xrecv[:, keep] = acc[mine, keep] + xrecv[:, keep]
        arrived(yrecv, s_out + 1)
        rows = out_ref.shape[0]
        out_ref[...] = (xrecv[:rows, keep] + yrecv[:rows, :].astype(F32)) * (1.0 / 4096.0)

    steps = []

    def at(t, fn, *args):
        steps.append((t, len(steps), functools.partial(fn, *args)))

    at(0, start)
    at(3, act_first)
    quads = [(0, 0), (0, 1), (1, 0), (1, 1)]
    for i, (a, f) in enumerate(quads):
        at(5 + 3 * i, y_to_x, g_place, s_gy, s_gx, a, f)
        at((18, 18.1, 21, 21.1)[i], x_near, g_place, s_gx, a, f)
        at(30, x_far, g_place, s_gx, a, f)
        at(24 + 0.1 * i, y_to_x, p_place, s_py, s_px, a, f)
        at(33 + 0.1 * i, x_near, p_place, s_px, a, f)
        at(43.9, x_far, p_place, s_px, a, f)
    for k, t in ((1, 7), (2, 11.5), (3, 14.5), (4, 17)):
        at(t, act_step, k)
    at(14.2, bt_forward)
    at(15, bt_ready)
    at(17.5, project_acts)
    at(17.6, y_start, paloc, p_place, s_py)
    for grp, t0, r0, a0 in ((0, 15.5, 19, 29), (1, 22, 26.1, 36), (2, 22.5, 26.2, 36.2), (3, 31, 34.5, 44)):
        at(t0, project, grp)
        at(t0 + 0.1, rs_step, grp, 0)
        for k in (1, 2, 3):
            at(r0 + 3.3 * (k - 1), rs_step, grp, k)
        at(a0, rs_last, grp)
        for k in (1, 2, 3, 4):
            at(a0 + 3 * k, ag_step, grp, k)
    at(44.5, squares, 0, True)
    at(49, squares, 1, False)
    at(49.5, squares, 2, False)
    at(57, squares, 3, False)
    at(60, out_core)
    at(61, out_y)
    for _, _, fn in sorted(steps, key=lambda s: (s[0], s[1])):
        fn()
    y_finish(gt_ref, g_place, s_gy)
    y_finish(paloc, p_place, s_py)
    for copy in sent:
        copy.wait_send()


def shards(activations, gradients, basis_in, basis_out):
    seq, feat = gradients.shape[1:]
    cols = basis_out.shape[1]
    width = basis_in.shape[1]
    half = (cols + 31) // 32 * 32
    chunk = half // 2
    gt = gradients[0].T
    bt = jnp.pad(basis_out.T, ((0, half - cols), (0, 0)))
    dims = (feat, seq, half, chunk, width)
    n_sems = 160
    return pl.pallas_call(
        functools.partial(kernel, dims),
        out_shape=jax.ShapeDtypeStruct((cols, width), F32),
        in_specs=[pl.BlockSpec(memory_space=pltpu.VMEM)] * 3 + [pl.BlockSpec(memory_space=pl.ANY)],
        out_specs=pl.BlockSpec(memory_space=pltpu.VMEM),
        scratch_shapes=[
            pltpu.VMEM((NYL, 2 * half, feat), BF16),
            pltpu.VMEM((4, NYL, feat, 2 * seq), BF16),
            pltpu.VMEM((NYL, NZ, seq, width), BF16),
            pltpu.VMEM(basis_in.shape, BF16),
            pltpu.VMEM((seq, width), BF16),
            pltpu.VMEM((4, 2 * seq, 2 * width), BF16),
            pltpu.VMEM((4, NZ, chunk, seq), BF16),
            pltpu.VMEM((4, NZ, chunk, seq), BF16),
            pltpu.VMEM((4, NZ * chunk, seq), BF16),
            pltpu.VMEM((2 * half, 2 * width), F32),
            pltpu.VMEM((half, 2 * width), F32),
            pltpu.VMEM((half, width), BF16),
            pltpu.VMEM((half, width), BF16),
            pltpu.SemaphoreType.DMA((n_sems,)),
            pltpu.SemaphoreType.DMA((n_sems,)),
        ],
        compiler_params=pltpu.CompilerParams(
            collective_id=0, has_side_effects=True, vmem_limit_bytes=48 * 1024 * 1024
        ),
        name="ekfac",
    )(gt, bt, activations[0], basis_in)


def solution(mesh):
    return jax.shard_map(
        shards,
        mesh=mesh,
        in_specs=(P("dp", None, "mp"), P("dp", None, "mp"), P(None, "mp"), P("mp", "dp")),
        out_specs=P("dp", "mp"),
        check_vma=False,
    )
```

time: 299 us -> 109 us (0.36)
  the two profiles are of different devices: /device:TPU:2 before, /device:TPU:1 now
where the time goes in v1:
time: 109 us
  Pallas kernels  104 us (95%)
  local copies, waits for them, and re-layouts  4.23 us (4%)
    pallas_call x1, Pallas kernels, shards(): pl.pallas_call(functools.partial(kernel, dims), out_shape=jax.ShapeDtypeS...  104 us
    unnamed x8, local copies, waits for them, and re-layouts  4.18 us

profile of v1, /device:TPU:1, one launch (start us, length us, event | category | flops | bytes accessed | tf_op | source)
XLA Modules:
  0.0 108.6 jit_solution(797528845560095013)
XLA Ops:
  0.0 0.0 copy-start
  0.0 1.4 %copy.5 = bf16[688,344]{0,1:T(8,128)(2,1)S(1)} copy(bf16[688,344]{1,0:T(8,128)(2,1)} %param.7) | data formatting | bytes 946688 | tf_op args[3]
  1.4 0.1 pad.4.bt_ref
  1.5 0.3 copy-done
  1.8 0.0 copy-start.1
  1.8 0.9 copy-done.1
  2.7 0.0 copy-start.2
  2.7 0.8 copy-done.2
  3.5 104.3 %ekfac.1 = f32[344,256]{1,0:T(8,128)S(1)} custom-call(bf16[688,128]{1,0:T(8,128)(2,1)S(1)} %bitcast.5, bf16[352,688]{1,0:T(8,128)(2,1)S(1)} %pad.4.bt_ref, bf16[128,256]{1,0:T(8,128)(2,1)S(1)} %bitcast.6, bf16[4096,256]{1,0:T(8,128)(2,1)S(1)} %copy-done), custom_call_target="tpu_custom_call" | custom-call | tf_op jit(solution)/shard_map/ekfac/pallas_call | solution.py:317
  107.8 0.7 copy.7
Async XLA Ops:
  0.0 1.7 %copy-start = (bf16[4096,256]{1,0:T(8,128)(2,1)S(1)}, bf16[4096,256]{1,0:T(8,128)(2,1)}, u32[]{:S(2)}) copy-start(bf16[4096,256]{1,0:T(8,128)(2,1)} %bin_hbm.1) | copy-start | bytes 6291460
  1.8 0.9 copy-start.1
  2.7 0.8 copy-start.2

commit v2 on v1

v2 whole, which is shorter than its diff:
```python
import functools

import jax
import jax.numpy as jnp
from jax import lax
from jax.experimental import pallas as pl
from jax.experimental.pallas import tpu as pltpu
from jax.sharding import PartitionSpec as P

MESH = pl.DeviceIdType.MESH
NX, NYH, NYL, NZ = 4, 4, 2, 8
F32, BF16 = jnp.float32, jnp.bfloat16
PAIRS = (((0, 0), (1, 0)), ((2, 0), (0, 1)), ((3, 0), (1, 1)), ((2, 1), (3, 1)))
HOME = {pair[h]: (p, h) for p, pair in enumerate(PAIRS) for h in range(2)}


def kernel(
    dims, bt_ref, gt_hbm, act_hbm, bin_hbm, out_ref,
    bt, gt, g, act, binv, paloc, pa, part, rsb, pg, acc, xrecv, ysend, yrecv,
    send_sems, recv_sems, loc_sems,
):
    feat, seq, half, chunk, width = dims
    dp, mp = lax.axis_index("dp"), lax.axis_index("mp")
    core, x, yh = dp % 2, (dp // 2) % NX, dp // (2 * NX)
    yl, z = mp // NZ, mp % NZ

    def dev(yh_=None, x_=None, c_=None, yl_=None, z_=None):
        yh_ = yh if yh_ is None else yh_
        x_ = x if x_ is None else x_
        c_ = core if c_ is None else c_
        yl_ = yl if yl_ is None else yl_
        z_ = z if z_ is None else z_
        return ((yh_ * NX + x_) * 2 + c_, yl_ * NZ + z_)

    sibling = dev(c_=1 - core)
    ypart = dev(yl_=1 - yl)
    xn = {1: dev(x_=(x + 1) % NX), -1: dev(x_=(x + NX - 1) % NX)}
    zn = {k: dev(z_=(z + NZ + k) % NZ) for k in (1, -1, 2, -2)}

    y = yh * NYL + yl
    ny = NYH * NYL

    def ydev(k):
        yy = (y + ny + k) % ny
        return dev(yh_=yy // NYL, yl_=yy % NYL)

    sigma = 1 - 2 * (yh % 2)
    inner = yl == yh % 2
    outer = yl != yh % 2

    def own_block():
        p, h = HOME[0, 0]
        return g.at[p, 0, :, h * seq:(h + 1) * seq]

    pltpu.make_async_copy(gt_hbm, gt, loc_sems.at[0]).start()
    pltpu.make_async_copy(act_hbm, act.at[0, z], loc_sems.at[1]).start()
    pltpu.make_async_copy(bin_hbm, binv, loc_sems.at[2]).start()
    pl.when(inner)(lambda: pltpu.make_async_copy(gt_hbm, own_block(), loc_sems.at[3]).start())

    barrier = pltpu.get_barrier_semaphore()
    peers = [sibling, xn[1], xn[-1], zn[1], zn[-1], zn[2], zn[-2], ydev(1), ydev(-1), ydev(2), ydev(-2)]
    for peer in peers:
        pl.semaphore_signal(barrier, inc=1, device_id=peer, device_id_type=MESH)
    pl.semaphore_wait(barrier, len(peers))

    counter = [0]
    sent = []

    def take(n=1):
        base = counter[0]
        counter[0] += n
        return base

    def copy_to(src, dst, ssem, rsem, to):
        return pltpu.make_async_remote_copy(
            src_ref=src, dst_ref=dst, send_sem=send_sems.at[ssem], recv_sem=recv_sems.at[rsem],
            device_id=to, device_id_type=MESH,
        )

    def send(src, dst, ssem, rsem, to):
        copy = copy_to(src, dst, ssem, rsem, to)
        copy.start()
        sent.append(copy)

    def send_when(cond, src, dst, ssem, rsem, to):
        copy = copy_to(src, dst, ssem, rsem, to)
        pl.when(cond)(copy.start)
        sent.append((cond, copy))

    def arrived(dst, rsem):
        pltpu.make_async_copy(dst, dst, recv_sems.at[rsem]).wait()

    s_bt = take(6)
    s_act0 = take(1)
    s_gy, s_gx = take(10), take(16)
    s_py, s_px = take(10), take(16)
    s_actz = take(16)
    s_rs, s_ag = take(32), take(32)
    s_out = take(4)

    def y_start(src, src_half, place, base):
        send_when(outer, src, place(0, 0, 1), base, base, ydev(1))
        send_when(outer, src, place(0, 0, 1), base + 1, base, ydev(-1))
        send_when(inner, src, place(0, 0, 0), base, base + 1, ydev(2 * sigma))
        send_when(inner, src_half(0), place(0, 1, 0, 0), base + 1, base + 3, ydev(-2 * sigma))
        send_when(inner, src_half(1), place(0, 1, 0, 1), base + 2, base + 4, ydev(-2 * sigma))

    def x_send(place, xbase, a, f):
        for d, slot in ((1, 1), (-1, 2)):
            s = xbase + slot * 4 + a * 2 + f
            send(place(0, a, f), place(slot, a, f), s, s, xn[d])

    def y_near_other(place, base, xbase):
        arrived(place(0, 0, 1), base)
        send(place(0, 0, 1), place(0, 1, 1), base + 3, base + 2, ydev(-2 * sigma))
        x_send(place, xbase, 0, 1)

    def y_near_own_inner(place, xbase, ready):
        def go():
            ready()
            for d, slot in ((1, 1), (-1, 2)):
                s = xbase + slot * 4
                copy_to(place(0, 0, 0), place(slot, 0, 0), s, s, xn[d]).start()

        pl.when(inner)(go)

    def y_near_own_outer(place, base, xbase):
        def go():
            arrived(place(0, 0, 0), base + 1)
            copy_to(place(0, 0, 0, 0), place(0, 1, 0, 0), base + 4, base + 3, ydev(-2 * sigma)).start()
            for d, slot in ((1, 1), (-1, 2)):
                s = xbase + slot * 4
                copy_to(place(0, 0, 0), place(slot, 0, 0), s, s, xn[d]).start()

        pl.when(outer)(go)
        sent.append((outer, copy_to(place(0, 0, 0, 0), place(0, 1, 0, 0), base + 4, base + 3, ydev(-2 * sigma))))
        for d, slot in ((1, 1), (-1, 2)):
            s = xbase + slot * 4
            sent.append(copy_to(place(0, 0, 0), place(slot, 0, 0), s, s, xn[d]))

    def y_far_other(place, base, xbase):
        arrived(place(0, 1, 1), base + 2)
        x_send(place, xbase, 1, 1)

    def y_far_own(place, base, xbase):
        arrived(place(0, 1, 0, 1), base + 4)
        send_when(outer, place(0, 1, 0, 1), place(0, 1, 0, 1), base + 5, base + 4, ydev(2 * sigma))
        arrived(place(0, 1, 0, 0), base + 3)
        x_send(place, xbase, 1, 0)

    def x_near(place, xbase, a, f):
        for d, slot in ((1, 1), (-1, 2)):
            arrived(place(slot, a, f), xbase + slot * 4 + a * 2 + f)
            if f == slot - 1:
                s = xbase + 12 + a * 2 + f
                send(place(slot, a, f), place(3, a, f), s, s, xn[d])

    def x_far(place, xbase, a, f):
        arrived(place(3, a, f), xbase + 12 + a * 2 + f)

    cut = (feat // 2 + 15) // 16 * 16
    g_parts = {None: slice(None), 0: slice(0, cut), 1: slice(cut, feat)}
    p_parts = {None: (0, seq), 0: (0, seq // 2), 1: (seq // 2, seq)}

    def g_place(slot, a, f, part_=None):
        p, h = HOME[slot, a]
        return g.at[p, f, g_parts[part_], h * seq:(h + 1) * seq]

    def p_place(slot, a, f, part_=None):
        lo, hi = p_parts[part_]
        return pa.at[slot, a * seq + lo:a * seq + hi, f * width:(f + 1) * width]

    def gt_half(i):
        return gt.at[g_parts[i], :]

    def paloc_half(i):
        return paloc.at[slice(*p_parts[i]), :]

    def bt_place(f, c, i):
        return bt.at[f, pl.ds(pl.multiple_of(c * half + i * chunk, 16), chunk), :]

    def bt_src(i):
        return bt_ref.at[i * chunk:(i + 1) * chunk, :]

    def start():
        pltpu.make_async_copy(act_hbm, act.at[0, z], loc_sems.at[1]).wait()
        send(act.at[0, z], act.at[1, z], s_act0, s_act0, ypart)
        pltpu.make_async_copy(gt_hbm, gt, loc_sems.at[0]).wait()
        y_start(gt, gt_half, g_place, s_gy)

    def own_ready():
        pltpu.make_async_copy(gt_hbm, own_block(), loc_sems.at[3]).wait()

    def bt_send(i):
        send(bt_src(i), bt_place(1, core, i), s_bt + 2 + i, s_bt + 2 + i, ypart)
        send(bt_src(i), bt_place(0, core, i), s_bt + i, s_bt + i, sibling)

    def bt_own():
        bt[0, pl.ds(pl.multiple_of(core * half, 16), half), :] = bt_ref[...]

    def bt_forward(i):
        arrived(bt_place(1, core, i), s_bt + 2 + i)
        send(bt_place(1, core, i), bt_place(1, core, i), s_bt + 4 + i, s_bt + 4 + i, sibling)

    def bt_ready():
        for i in range(2):
            arrived(bt_place(0, 1 - core, i), s_bt + i)
            arrived(bt_place(1, 1 - core, i), s_bt + 4 + i)

    def act_send(f, owner, k, tag):
        send(act.at[f, owner], act.at[f, owner], s_actz + tag, s_actz + tag, zn[k])

    def act_tag(f, d, dist):
        return f * 8 + (0 if d == 1 else 4) + dist - 1

    def act_first(f):
        if f == 1:
            arrived(act.at[1, z], s_act0)
        for dist in (2, 1):
            for d in (1, -1):
                act_send(f, z, d * dist, act_tag(f, d, dist))

    def act_wait(f, d, dist):
        arrived(act.at[f, (z + NZ - d * dist) % NZ], s_actz + act_tag(f, d, dist))

    def act_forward():
        for f in range(2):
            for d in (1, -1):
                act_wait(f, d, 2)
                owner = (z + NZ - 2 * d) % NZ
                if (f == 0) == (d == 1):
                    act_send(f, owner, 2 * d, act_tag(f, d, 4))
                act_send(f, owner, d, act_tag(f, d, 3))

    def act_rest():
        for dist in (1, 3, 4):
            for f in range(2):
                for d in (1, -1):
                    if dist < 4 or (f == 0) == (d == 1):
                        act_wait(f, d, dist)

    def project_acts():
        pltpu.make_async_copy(bin_hbm, binv, loc_sems.at[2]).wait()
        total = jnp.zeros((seq, width), F32)
        for f in range(2):
            low = (yl if f == 0 else 1 - yl) * NZ

            def body(i, total, f=f, low=low):
                rows = pl.ds(pl.multiple_of((low + i) * width, 128), width)
                return total + jnp.dot(act[f, i], binv[rows, :], preferred_element_type=F32)

            total = lax.fori_loop(0, NZ, body, total)
        paloc[...] = total.astype(BF16)

        def keep():
            pa[0, :seq, :width] = total.astype(BF16)

        pl.when(inner)(keep)

    def pa_start():
        y_start(paloc, paloc_half, p_place, s_py)

    def project(grp):
        def body(r, carry):
            rows = pl.ds(pl.multiple_of(r * chunk, 16), chunk)
            t = jnp.dot(bt[0, rows, :], g[grp, 0], preferred_element_type=F32)
            t = t + jnp.dot(bt[1, rows, :], g[grp, 1], preferred_element_type=F32)
            t = t.astype(BF16)
            part[grp, r] = t[:, :seq]
            part[grp, r + 4] = t[:, seq:]
            return carry

        lax.fori_loop(0, 4, body, 0)

    def rlen(grp, d):
        return 4 if (grp % 2 == 0) == (d == 1) else 3

    def rs_slot(d, k):
        return (0 if d == 1 else 4) + k

    def rs_step(grp, k):
        for d in (1, -1):
            n = rlen(grp, d)
            if k < n:
                j = (z + NZ + d * (n - k)) % NZ
                if k == 0:
                    src = part.at[grp, j]
                else:
                    slot = rs_slot(d, k - 1)
                    src = rsb.at[grp, slot]
                    arrived(src, s_rs + grp * 8 + slot)
                    rsb[grp, slot] = (rsb[grp, slot].astype(F32) + part[grp, j].astype(F32)).astype(BF16)
                s = s_rs + grp * 8 + rs_slot(d, k)
                send(src, rsb.at[grp, rs_slot(d, k)], s, s, zn[d])

    def pg_place(grp, j):
        return pg.at[grp, pl.ds(pl.multiple_of(j * chunk, 16), chunk), :]

    def ag_sem(grp, d, k):
        return s_ag + grp * 8 + rs_slot(d, k)

    def rs_last(grp):
        total = part[grp, z].astype(F32)
        for d in (1, -1):
            slot = rs_slot(d, rlen(grp, d) - 1)
            arrived(rsb.at[grp, slot], s_rs + grp * 8 + slot)
            total = total + rsb[grp, slot].astype(F32)
        pg[grp, pl.ds(pl.multiple_of(z * chunk, 16), chunk), :] = total.astype(BF16)
        for d in (1, -1):
            send(pg_place(grp, z), pg_place(grp, z), ag_sem(grp, d, 0), ag_sem(grp, d, 0), zn[d])

    def ag_step(grp, k):
        for d in (1, -1):
            n = rlen(grp, d)
            if k <= n:
                j = (z + NZ - d * k) % NZ
                arrived(pg_place(grp, j), ag_sem(grp, d, k - 1))
                if k < n:
                    send(pg_place(grp, j), pg_place(grp, j), ag_sem(grp, d, k), ag_sem(grp, d, k), zn[d])

    def squares(grp, lo, hi):
        def body(r, carry):
            rows = pl.ds(pl.multiple_of(r * chunk, 16), chunk)
            total = None if grp == 0 else acc[rows, lo:hi]
            for a in range(2):
                lhs = pg[grp, pl.ds(pl.multiple_of((a * 4 + r) * chunk, 16), chunk), :]
                slot, far = PAIRS[grp][a]
                t = jnp.dot(lhs, pa[slot, far * seq:(far + 1) * seq, lo:hi], preferred_element_type=F32)
                total = t * t if total is None else total + t * t
            acc[rows, lo:hi] = total
            return carry

        lax.fori_loop(0, 4, body, 0)

    mine = pl.ds(pl.multiple_of(core * half, 8), half)
    theirs = pl.ds(pl.multiple_of((1 - core) * half, 8), half)
    spans = (slice(0, width), slice(width, 2 * width))

    def out_core(i):
        send(acc.at[theirs, spans[i]], xrecv.at[:, spans[i]], s_out + i, s_out + i, sibling)

    def out_y():
        arrived(xrecv.at[:, spans[1]], s_out + 1)
        for i in range(2):
            rows = slice(i * chunk, (i + 1) * chunk)
            ysend[rows, :] = (acc[pl.ds(pl.multiple_of(core * half + i * chunk, 8), chunk), spans[1]]
                              + xrecv[rows, spans[1]]).astype(BF16)
            send(ysend.at[rows, :], yrecv.at[rows, :], s_out + 2 + i, s_out + 2 + i, ypart)

    def out_last():
        arrived(xrecv.at[:, spans[0]], s_out)
        total = out_ref.shape[0]
        for i in range(2):
            lo, hi = i * chunk, min((i + 1) * chunk, total)
            arrived(yrecv.at[lo:(i + 1) * chunk, :], s_out + 2 + i)
            own = acc[pl.ds(pl.multiple_of(core * half + lo, 8), hi - lo), spans[0]] + xrecv[lo:hi, spans[0]]
            out_ref[lo:hi, :] = (own + yrecv[lo:hi, :].astype(F32)) * (1.0 / 4096.0)

    steps = []

    def at(t, fn, *args):
        steps.append((t, len(steps), functools.partial(fn, *args)))

    at(0, start)
    at(0.05, act_first, 0)
    at(0.1, y_near_own_inner, g_place, s_gx, own_ready)
    at(0.2, bt_send, 0)
    at(0.3, bt_own)
    at(4, act_first, 1)
    at(6.5, y_near_other, g_place, s_gy, s_gx)
    at(6.6, bt_send, 1)
    at(9, y_near_own_outer, g_place, s_gy, s_gx)
    at(13, x_near, g_place, s_gx, 0, 0)
    at(13.1, x_near, g_place, s_gx, 0, 1)
    at(14, bt_forward, 0)
    at(16.5, act_forward)
    at(17, y_far_other, g_place, s_gy, s_gx)
    at(20, y_far_own, g_place, s_gy, s_gx)
    at(22, bt_forward, 1)
    at(24, bt_ready)
    at(24.1, project, 0)
    at(24.1, rs_step, 0, 0)
    at(24.2, project, 1)
    at(24.2, rs_step, 1, 0)
    at(25.1, x_near, g_place, s_gx, 1, 1)
    at(25.2, act_rest)
    at(25.3, project_acts)
    at(25.4, pa_start)
    at(27, x_near, g_place, s_gx, 1, 0)
    at(27.9, x_far, g_place, s_gx, 0, 0)
    at(27.9, x_far, g_place, s_gx, 0, 1)
    at(28, project, 2)
    at(28, rs_step, 2, 0)
    at(32, x_far, g_place, s_gx, 1, 0)
    at(32, x_far, g_place, s_gx, 1, 1)
    at(32, project, 3)
    at(32, rs_step, 3, 0)
    at(31, y_near_own_inner, p_place, s_px, lambda: None)
    at(31.1, y_near_other, p_place, s_py, s_px)
    at(31.2, y_near_own_outer, p_place, s_py, s_px)
    at(36, y_far_other, p_place, s_py, s_px)
    at(36.1, y_far_own, p_place, s_py, s_px)
    for i, (a, f) in enumerate(((0, 0), (0, 1), (1, 1), (1, 0))):
        at(41 + 0.1 * i, x_near, p_place, s_px, a, f)
        at(46.5, x_far, p_place, s_px, a, f)
    for grp, r0, a0 in ((0, 27.5, 38), (1, 27.8, 38.3), (2, 31.8, 42.3), (3, 36, 46.5)):
        for k in (1, 2, 3):
            at(r0 + 3.5 * (k - 1), rs_step, grp, k)
        at(a0, rs_last, grp)
        for k in (1, 2, 3, 4):
            at(a0 + 3.5 * k, ag_step, grp, k)
    at(53, squares, 0, 0, 2 * width)
    at(54, squares, 1, 0, 2 * width)
    at(57.1, squares, 2, 0, 2 * width)
    at(62, squares, 3, width, 2 * width)
    at(62.1, out_core, 1)
    at(62.2, squares, 3, 0, width)
    at(62.3, out_core, 0)
    at(63, out_y)
    at(64, out_last)
    for _, _, fn in sorted(steps, key=lambda s: (s[0], s[1])):
        fn()
    for item in sent:
        if isinstance(item, tuple):
            pl.when(item[0])(item[1].wait_send)
        else:
            item.wait_send()


def shards(activations, gradients, basis_in, basis_out):
    seq, feat = gradients.shape[1:]
    cols = basis_out.shape[1]
    width = basis_in.shape[1]
    half = (cols + 31) // 32 * 32
    chunk = half // 2
    gt = gradients[0].T
    bt = jnp.pad(basis_out.T, ((0, half - cols), (0, 0)))
    dims = (feat, seq, half, chunk, width)
    n_sems = 184
    return pl.pallas_call(
        functools.partial(kernel, dims),
        out_shape=jax.ShapeDtypeStruct((cols, width), F32),
        in_specs=[pl.BlockSpec(memory_space=pltpu.VMEM)] + [pl.BlockSpec(memory_space=pltpu.HBM)] * 3,
        out_specs=pl.BlockSpec(memory_space=pltpu.VMEM),
        scratch_shapes=[
            pltpu.VMEM((NYL, 2 * half, feat), BF16),
            pltpu.VMEM((feat, seq), BF16),
            pltpu.VMEM((4, NYL, feat, 2 * seq), BF16),
            pltpu.VMEM((NYL, NZ, seq, width), BF16),
            pltpu.VMEM(basis_in.shape, BF16),
            pltpu.VMEM((seq, width), BF16),
            pltpu.VMEM((4, 2 * seq, 2 * width), BF16),
            pltpu.VMEM((4, NZ, chunk, seq), BF16),
            pltpu.VMEM((4, NZ, chunk, seq), BF16),
            pltpu.VMEM((4, NZ * chunk, seq), BF16),
            pltpu.VMEM((2 * half, 2 * width), F32),
            pltpu.VMEM((half, 2 * width), F32),
            pltpu.VMEM((half, width), BF16),
            pltpu.VMEM((half, width), BF16),
            pltpu.SemaphoreType.DMA((n_sems,)),
            pltpu.SemaphoreType.DMA((n_sems,)),
            pltpu.SemaphoreType.DMA((4,)),
        ],
        compiler_params=pltpu.CompilerParams(
            collective_id=0, has_side_effects=True, vmem_limit_bytes=60 * 1024 * 1024
        ),
        name="ekfac",
    )(bt, gt, activations[0], basis_in)


def solution(mesh):
    return jax.shard_map(
        shards,
        mesh=mesh,
        in_specs=(P("dp", None, "mp"), P("dp", None, "mp"), P(None, "mp"), P("mp", "dp")),
        out_specs=P("dp", "mp"),
        check_vma=False,
    )
```

time: 109 us -> 102 us (0.936)
  Pallas kernels: 104 us -> 97.8 us
    pallas_call x1, Pallas kernels: 104 us -> 97.8 us  [shards(): pl.pallas_call(functools.partial(kernel, dims), out_shape=jax.ShapeDtypeS...]
    unnamed x8 -> x2, local copies, waits for them, and re-layouts: 4.18 us -> 3 us
where the time goes in v2:
time: 102 us
  Pallas kernels  97.8 us (96%)
  local copies, waits for them, and re-layouts  3.84 us (4%)
    pallas_call x1, Pallas kernels, shards(): pl.pallas_call(functools.partial(kernel, dims), out_shape=jax.ShapeDtypeS...  97.8 us
    unnamed x2, local copies, waits for them, and re-layouts  3 us

profile of v2, /device:TPU:1, one launch (start us, length us, event | category | flops | bytes accessed | tf_op | source)
XLA Modules:
  0.0 101.7 jit_solution(7080824946085705742)
XLA Ops:
  0.0 1.3 %copy.5 = bf16[688,344]{0,1:T(8,128)(2,1)S(1)} copy(bf16[688,344]{1,0:T(8,128)(2,1)} %param.7) | data formatting | bytes 946688 | tf_op args[3]
  1.3 0.8 pad.4.bt_ref
  2.1 97.8 %ekfac.1 = f32[344,256]{1,0:T(8,128)} custom-call(bf16[352,688]{1,0:T(8,128)(2,1)} %pad.4.bt_ref, bf16[688,128]{1,0:T(8,128)(2,1)} %bitcast.6, bf16[128,256]{1,0:T(8,128)(2,1)} %bitcast.7, bf16[4096,256]{1,0:T(8,128)(2,1)} %bin_hbm.1), custom_call_target="tpu_custom_call" | custom-call | tf_op jit(solution)/shard_map/ekfac/pallas_call | solution.py:440
  99.9 1.7 %copy.7 = f32[344,256]{1,0:T(8,128)} copy(f32[344,256]{1,0:T(8,128)} %ekfac.1) | data formatting | bytes 704512

commit v3 on v2

v3 whole, which is shorter than its diff:
```python
import functools

import jax
import jax.numpy as jnp
from jax import lax
from jax.experimental import pallas as pl
from jax.experimental.pallas import tpu as pltpu
from jax.sharding import PartitionSpec as P

MESH = pl.DeviceIdType.MESH
NX, NYH, NYL, NZ = 4, 4, 2, 8
F32, BF16 = jnp.float32, jnp.bfloat16
SETS = (((0, 0), (1, 0), (2, 0), (0, 1)), ((3, 0), (1, 1), (2, 1), (3, 1)))
HOME = {key: (k, pos) for k, keys in enumerate(SETS) for pos, key in enumerate(keys)}


def kernel(
    dims, basis_hbm, gt_hbm, act_hbm, bin_hbm, out_ref,
    raw, bt, gt, g, act, binv, paloc, pa, part, rsb, pg, acc, xrecv, ysend, yrecv,
    send_sems, recv_sems, loc_sems,
):
    feat, seq, half, chunk, width = dims
    dp, mp = lax.axis_index("dp"), lax.axis_index("mp")
    core, x, yh = dp % 2, (dp // 2) % NX, dp // (2 * NX)
    yl, z = mp // NZ, mp % NZ

    def dev(yh_=None, x_=None, c_=None, yl_=None, z_=None):
        yh_ = yh if yh_ is None else yh_
        x_ = x if x_ is None else x_
        c_ = core if c_ is None else c_
        yl_ = yl if yl_ is None else yl_
        z_ = z if z_ is None else z_
        return ((yh_ * NX + x_) * 2 + c_, yl_ * NZ + z_)

    sibling = dev(c_=1 - core)
    ypart = dev(yl_=1 - yl)
    xn = {1: dev(x_=(x + 1) % NX), -1: dev(x_=(x + NX - 1) % NX)}
    zn = {k: dev(z_=(z + NZ + k) % NZ) for k in (1, -1, 2, -2)}

    y = yh * NYL + yl
    ny = NYH * NYL

    def ydev(k):
        yy = (y + ny + k) % ny
        return dev(yh_=yy // NYL, yl_=yy % NYL)

    sigma = 1 - 2 * (yh % 2)
    inner = yl == yh % 2
    outer = yl != yh % 2

    def own_block():
        return g.at[0, 0, :, :seq]

    pltpu.make_async_copy(gt_hbm, gt, loc_sems.at[0]).start()
    pltpu.make_async_copy(act_hbm, act.at[0, z], loc_sems.at[1]).start()
    pltpu.make_async_copy(basis_hbm, raw, loc_sems.at[4]).start()
    pltpu.make_async_copy(bin_hbm, binv, loc_sems.at[2]).start()
    pl.when(inner)(lambda: pltpu.make_async_copy(gt_hbm, own_block(), loc_sems.at[3]).start())

    barrier = pltpu.get_barrier_semaphore()
    peers = [sibling, xn[1], xn[-1], zn[1], zn[-1], zn[2], zn[-2], ydev(1), ydev(-1), ydev(2), ydev(-2)]
    for peer in peers:
        pl.semaphore_signal(barrier, inc=1, device_id=peer, device_id_type=MESH)
    pl.semaphore_wait(barrier, len(peers))

    refs = (basis_hbm, gt_hbm, act_hbm, bin_hbm, out_ref, raw, bt, gt, g, act, binv, paloc, pa, part, rsb, pg, acc,
            xrecv, ysend, yrecv, send_sems, recv_sems, loc_sems)
    where = (core, yl, z, sigma, sibling, ypart, xn, zn, ydev, own_block)
    pl.when(inner)(lambda: program(True, dims, where, *refs))
    pl.when(outer)(lambda: program(False, dims, where, *refs))


def program(
    is_inner, dims, where, basis_hbm, gt_hbm, act_hbm, bin_hbm, out_ref, raw, bt, gt, g, act, binv, paloc, pa, part,
    rsb, pg, acc, xrecv, ysend, yrecv, send_sems, recv_sems, loc_sems,
):
    feat, seq, half, chunk, width = dims
    core, yl, z, sigma, sibling, ypart, xn, zn, ydev, own_block = where
    counter = [0]

    def take(n=1):
        base = counter[0]
        counter[0] += n
        return base

    S_GY, S_GX, S_PY, S_PX, S_ACT, S_BT, S_RS, S_AG, S_OC, S_OY = range(10)

    def send(src, dst, kind, rsem, to):
        pltpu.make_async_remote_copy(
            src_ref=src, dst_ref=dst, send_sem=send_sems.at[kind], recv_sem=recv_sems.at[rsem],
            device_id=to, device_id_type=MESH,
        ).start()

    def arrived(dst, rsem):
        pltpu.make_async_copy(dst, dst, recv_sems.at[rsem]).wait()

    s_bt = take(6)
    s_act0 = take(1)
    s_gy, s_gx = take(8), take(24)
    s_py, s_px = take(8), take(12)
    s_actz = take(16)
    s_rs, s_ag = take(32), take(32)
    s_out = take(6)

    def num(part):
        return 1 if part == 1 else 0

    def y_start(pat):
        place, source, parts, base, _, kind, _ = pat

        def from_outer():
            for p in parts:
                for d in (1, -1):
                    send(source(p), place(0, 0, 1, p), kind, base + num(p), ydev(d))

        def from_inner():
            for p in parts:
                send(source(p), place(0, 0, 0, p), kind, base + 2 + num(p), ydev(2 * sigma))
                for h in (0, 1) if p is None else (p,):
                    send(source(h), place(0, 1, 0, h), kind, base + 6 + h, ydev(-2 * sigma))

        from_inner() if is_inner else from_outer()

    def x_send(pat, a, f, p):
        place, _, parts, _, base, _, kind = pat
        for d, slot in ((1, 1), (-1, 2)):
            s = base + ((slot - 1) * 4 + a * 2 + f) * len(parts) + num(p)
            send(place(0, a, f, p), place(slot, a, f, p), kind, s, xn[d])

    def y_near_other(pat, p):
        place, _, _, base, _, kind, _ = pat
        arrived(place(0, 0, 1, p), base + num(p))
        send(place(0, 0, 1, p), place(0, 1, 1, p), kind, base + 4 + num(p), ydev(-2 * sigma))
        x_send(pat, 0, 1, p)

    def y_near_own(pat):
        place, _, parts, base, _, kind, _ = pat
        for p in parts:
            if not is_inner:
                arrived(place(0, 0, 0, p), base + 2 + num(p))
                if p != 1:
                    send(place(0, 0, 0, 0), place(0, 1, 0, 0), kind, base + 6, ydev(-2 * sigma))
            x_send(pat, 0, 0, p)

    def y_far_own(pat):
        place, _, parts, base, _, kind, _ = pat
        for h in (1, 0):
            arrived(place(0, 1, 0, h), base + 6 + h)
            if not is_inner and h == 1:
                send(place(0, 1, 0, 1), place(0, 1, 0, 1), kind, base + 7, ydev(2 * sigma))
            if h in parts:
                x_send(pat, 1, 0, h)
        if None in parts:
            x_send(pat, 1, 0, None)

    def y_far_other(pat, p):
        place, _, _, base, _, _, _ = pat
        arrived(place(0, 1, 1, p), base + 4 + num(p))
        x_send(pat, 1, 1, p)

    def x_near(pat, a, f):
        place, _, parts, _, base, _, kind = pat
        for p in parts:
            for d, slot in ((1, 1), (-1, 2)):
                s = base + ((slot - 1) * 4 + a * 2 + f) * len(parts) + num(p)
                arrived(place(slot, a, f, p), s)
                if f == slot - 1:
                    s = base + (8 + a * 2 + f) * len(parts) + num(p)
                    send(place(slot, a, f, p), place(3, a, f, p), kind, s, xn[d])

    def x_far(pat, a, f):
        place, _, parts, _, base, _, _ = pat
        for p in parts:
            arrived(place(3, a, f, p), base + (8 + a * 2 + f) * len(parts) + num(p))

    cut = (feat // 2 + 15) // 16 * 16
    g_parts = {None: slice(None), 0: slice(0, cut), 1: slice(cut, feat)}
    p_parts = {None: (0, seq), 0: (0, seq // 2), 1: (seq // 2, seq)}

    def g_place(slot, a, f, part_=None):
        k, pos = HOME[slot, a]
        return g.at[k, f, g_parts[part_], pos * seq:(pos + 1) * seq]

    def p_place(slot, a, f, part_=None):
        lo, hi = p_parts[part_]
        return pa.at[slot, a * seq + lo:a * seq + hi, f * width:(f + 1) * width]

    def g_source(p):
        return gt.at[g_parts[p], :]

    def p_source(p):
        return paloc.at[slice(*p_parts[p]), :]

    gpat = (g_place, g_source, (0, 1), s_gy, s_gx, S_GY, S_GX)
    ppat = (p_place, p_source, (None,), s_py, s_px, S_PY, S_PX)

    def bt_place(f, c, i):
        return bt.at[f, pl.ds(pl.multiple_of(c * half + i * chunk, 16), chunk), :]

    def start():
        pltpu.make_async_copy(gt_hbm, gt, loc_sems.at[0]).wait()
        y_start(gpat)
        pltpu.make_async_copy(act_hbm, act.at[0, z], loc_sems.at[1]).wait()
        send(act.at[0, z], act.at[1, z], S_ACT, s_act0, ypart)

    def g_own():
        if is_inner:
            pltpu.make_async_copy(gt_hbm, own_block(), loc_sems.at[3]).wait()
        y_near_own(gpat)

    def bt_own():
        pltpu.make_async_copy(basis_hbm, raw, loc_sems.at[4]).wait()
        turned = raw[...].T
        bt[0, pl.ds(pl.multiple_of(core * half, 16), turned.shape[0]), :] = turned

    def bt_rows(f, lo, hi):
        return bt.at[f, pl.ds(pl.multiple_of(core * half + lo, 16), hi - lo), :]

    def bt_send(i, pieces=(0, 1)):
        split = chunk // 32 * 16
        for lo, hi in [((0, split), (split, chunk))[piece] for piece in pieces]:
            lo, hi = i * chunk + lo, i * chunk + hi
            send(bt_rows(0, lo, hi), bt_rows(1, lo, hi), S_BT, s_bt + 2 + i, ypart)
            send(bt_rows(0, lo, hi), bt_rows(0, lo, hi), S_BT, s_bt + i, sibling)

    def bt_forward(i):
        arrived(bt_place(1, core, i), s_bt + 2 + i)
        send(bt_place(1, core, i), bt_place(1, core, i), S_BT, s_bt + 4 + i, sibling)

    def bt_ready(i):
        arrived(bt_place(0, 1 - core, i), s_bt + i)
        arrived(bt_place(1, 1 - core, i), s_bt + 4 + i)

    def act_send(f, owner, k, tag):
        send(act.at[f, owner], act.at[f, owner], S_ACT, s_actz + tag, zn[k])

    def act_tag(f, d, dist):
        return f * 8 + (0 if d == 1 else 4) + dist - 1

    def act_first(f):
        if f == 1:
            arrived(act.at[1, z], s_act0)
        for dist in (2, 1):
            for d in (1, -1):
                act_send(f, z, d * dist, act_tag(f, d, dist))

    def act_wait(f, d, dist):
        arrived(act.at[f, (z + NZ - d * dist) % NZ], s_actz + act_tag(f, d, dist))

    def act_forward():
        for f in range(2):
            for d in (1, -1):
                act_wait(f, d, 2)
                owner = (z + NZ - 2 * d) % NZ
                if (f == 0) == (d == 1):
                    act_send(f, owner, 2 * d, act_tag(f, d, 4))
                act_send(f, owner, d, act_tag(f, d, 3))

    def act_rest():
        for dist in (1, 3, 4):
            for f in range(2):
                for d in (1, -1):
                    if dist < 4 or (f == 0) == (d == 1):
                        act_wait(f, d, dist)

    def project_acts():
        pltpu.make_async_copy(bin_hbm, binv, loc_sems.at[2]).wait()
        total = jnp.zeros((seq, width), F32)
        for f in range(2):
            low = (yl if f == 0 else 1 - yl) * NZ

            def body(i, total, f=f, low=low):
                rows = pl.ds(pl.multiple_of((low + i) * width, 128), width)
                return total + jnp.dot(act[f, i], binv[rows, :], preferred_element_type=F32)

            total = lax.fori_loop(0, NZ, body, total)
        paloc[...] = total.astype(BF16)

        if is_inner:
            pa[0, :seq, :width] = total.astype(BF16)

    def pa_start():
        y_start(ppat)

    def project(grp):
        a, i = grp // 2, grp % 2

        def body(c, carry):
            rows = pl.ds(pl.multiple_of(c * half + i * chunk, 16), chunk)
            for pair in range(2):
                cols = slice(2 * pair * seq, 2 * (pair + 1) * seq)
                t = jnp.dot(bt[0, rows, :], g[a, 0, :, cols], preferred_element_type=F32)
                t = t + jnp.dot(bt[1, rows, :], g[a, 1, :, cols], preferred_element_type=F32)
                t = t.astype(BF16)
                part[grp, c * 4 + 2 * pair] = t[:, :seq]
                part[grp, c * 4 + 2 * pair + 1] = t[:, seq:]
            return carry

        lax.fori_loop(0, 2, body, 0)

    def rlen(grp, d):
        return 4 if (grp % 2 == 0) == (d == 1) else 3

    def rs_slot(d, k):
        return (0 if d == 1 else 4) + k

    def rs_step(grp, k):
        for d in (1, -1):
            n = rlen(grp, d)
            if k < n:
                j = (z + NZ + d * (n - k)) % NZ
                if k == 0:
                    src = part.at[grp, j]
                else:
                    slot = rs_slot(d, k - 1)
                    src = rsb.at[grp, slot]
                    arrived(src, s_rs + grp * 8 + slot)
                    rsb[grp, slot] = (rsb[grp, slot].astype(F32) + part[grp, j].astype(F32)).astype(BF16)
                s = s_rs + grp * 8 + rs_slot(d, k)
                send(src, rsb.at[grp, rs_slot(d, k)], S_RS, s, zn[d])

    def pg_place(grp, j):
        return pg.at[grp, pl.ds(pl.multiple_of(j * chunk, 16), chunk), :]

    def ag_sem(grp, d, k):
        return s_ag + grp * 8 + rs_slot(d, k)

    def rs_last(grp):
        total = part[grp, z].astype(F32)
        for d in (1, -1):
            slot = rs_slot(d, rlen(grp, d) - 1)
            arrived(rsb.at[grp, slot], s_rs + grp * 8 + slot)
            total = total + rsb[grp, slot].astype(F32)
        pg[grp, pl.ds(pl.multiple_of(z * chunk, 16), chunk), :] = total.astype(BF16)
        for d in (1, -1):
            send(pg_place(grp, z), pg_place(grp, z), S_AG, ag_sem(grp, d, 0), zn[d])

    def ag_step(grp, k):
        for d in (1, -1):
            n = rlen(grp, d)
            if k <= n:
                j = (z + NZ - d * k) % NZ
                arrived(pg_place(grp, j), ag_sem(grp, d, k - 1))
                if k < n:
                    send(pg_place(grp, j), pg_place(grp, j), S_AG, ag_sem(grp, d, k), zn[d])

    def squares(grp, lo, hi):
        a, i = grp // 2, grp % 2

        def body(c, carry):
            rows = pl.ds(pl.multiple_of(c * half + i * chunk, 16), chunk)
            total = None if a == 0 else acc[rows, lo:hi]
            for pos, (slot, far) in enumerate(SETS[a]):
                lhs = pg[grp, pl.ds(pl.multiple_of((c * 4 + pos) * chunk, 16), chunk), :]
                t = jnp.dot(lhs, pa[slot, far * seq:(far + 1) * seq, lo:hi], preferred_element_type=F32)
                total = t * t if total is None else total + t * t
            acc[rows, lo:hi] = total
            return carry

        lax.fori_loop(0, 2, body, 0)

    spans = (slice(0, width), slice(width, 2 * width))

    def acc_rows(c, i):
        return pl.ds(pl.multiple_of(c * half + i * chunk, 8), chunk)

    def out_core(i, f):
        dst = xrecv.at[i * chunk:(i + 1) * chunk, spans[f]]
        send(acc.at[acc_rows(1 - core, i), spans[f]], dst, S_OC, s_out + 2 * i + f, sibling)

    def out_y(i):
        rows = slice(i * chunk, (i + 1) * chunk)
        arrived(xrecv.at[rows, spans[1]], s_out + 2 * i + 1)
        ysend[rows, :] = (acc[acc_rows(core, i), spans[1]] + xrecv[rows, spans[1]]).astype(BF16)
        send(ysend.at[rows, :], yrecv.at[rows, :], S_OY, s_out + 4 + i, ypart)

    def out_last(i):
        rows = slice(i * chunk, (i + 1) * chunk)
        n = min(chunk, out_ref.shape[0] - i * chunk)
        arrived(xrecv.at[rows, spans[0]], s_out + 2 * i)
        own = acc[acc_rows(core, i), spans[0]] + xrecv[rows, spans[0]]
        arrived(yrecv.at[rows, :], s_out + 4 + i)
        own = (own + yrecv[rows, :].astype(F32)) * (1.0 / 4096.0)
        out_ref[i * chunk:i * chunk + n, :] = own[:n]

    steps = []

    def at(t_inner, t_outer, fn, *args):
        steps.append((t_inner if is_inner else t_outer, len(steps), functools.partial(fn, *args)))

    at(0, 0, start)
    at(0.04, 11, g_own)
    at(0.05, 0.05, act_first, 0)
    at(0.3, 0.3, bt_own)
    at(0.35, 6.4, bt_send, 0, (0,))
    at(0.35, 11.2, bt_send, 0, (1,))
    at(0.36, 11.25, bt_send, 1)
    at(4, 4.5, y_near_other, gpat, 0)
    at(5.8, 6.3, y_near_other, gpat, 1)
    at(6.5, 15.5, x_near, gpat, 0, 0)
    at(15.45, 11.1, y_far_own, gpat)
    at(10.5, 12, x_near, gpat, 0, 1)
    at(11, 13, y_far_other, gpat, 0)
    at(12.5, 14.5, y_far_other, gpat, 1)
    at(12.6, 12.1, act_first, 1)
    at(15.3, 17, act_forward)
    at(15.5, 18.2, bt_forward, 0)
    at(28, 22.42, x_far, gpat, 0, 0)
    at(28, 22.42, x_far, gpat, 0, 1)
    at(15.4, 20.5, x_near, gpat, 1, 1)
    at(20.9, 18.5, x_near, gpat, 1, 0)
    at(18.5, 18.6, bt_ready, 0)
    at(18.6, 18.6, project, 0)
    at(18.6, 18.6, rs_step, 0, 0)
    at(21, 19, act_rest)
    at(21, 19, project_acts)
    at(21, 19, pa_start)
    at(22, 22.2, bt_forward, 1)
    at(25, 22.4, bt_ready, 1)
    at(25, 22.4, project, 1)
    at(25, 22.4, rs_step, 1, 0)
    at(28, 28, x_far, gpat, 1, 0)
    at(28, 28, x_far, gpat, 1, 1)
    for grp in (2, 3):
        at(28, 28, project, grp)
        at(28, 28, rs_step, grp, 0)
    at(22, 28.62, y_near_own, ppat)
    at(32.5, 28.61, y_near_other, ppat, None)
    at(41.1, 28.63, y_far_own, ppat)
    at(41, 41, y_far_other, ppat, None)
    for i, (a, f) in enumerate(((0, 0), (0, 1), (1, 1), (1, 0))):
        t = (43, 43, 47.4, 47.4)[i]
        at(t, t, x_near, ppat, a, f)
        t = (48, 48, 54.8, 54.8)[i]
        at(t, t, x_far, ppat, a, f)
    for grp, r0, a0 in ((0, 23, 34), (1, 29, 40.2), (2, 32, 43.3), (3, 32.1, 43.4)):
        for k in (1, 2, 3):
            t = r0 + 3.7 * (k - 1) + (2 if grp == 0 and k > 1 and not is_inner else 0)
            at(t, t, rs_step, grp, k)
        at(a0, a0, rs_last, grp)
        for k in (1, 2, 3, 4):
            t = a0 + 3.7 * k
            at(t, t, ag_step, grp, k)
    at(50, 50, squares, 0, 0, 2 * width)
    at(56, 56, squares, 1, 0, 2 * width)
    at(58.15, 58.15, squares, 2, 0, 2 * width)
    at(58.15, 58.15, out_core, 0, 1)
    at(58.15, 58.15, out_core, 0, 0)
    at(59, 59, squares, 3, width, 2 * width)
    at(59, 59, out_core, 1, 1)
    at(59.1, 59.1, squares, 3, 0, width)
    at(59.2, 59.2, out_core, 1, 0)
    at(59.3, 59.3, out_y, 0)
    at(61, 61, out_y, 1)
    at(62, 62, out_last, 0)
    at(63, 63, out_last, 1)

    def drain():
        def sent(ref, kind):
            pltpu.make_async_copy(ref, ref, send_sems.at[kind]).wait()

        blocks = 3 if is_inner else 4
        sent(g.at[0, 0, :, :blocks * seq], S_GY)
        sent(act.at[0, :blocks], S_PY)
        sent(g.at[:, :, :, seq:], S_GX)
        sent(pa.at[1:], S_PX)
        sent(binv.at[:15 * seq, :], S_ACT)
        sent(bt.at[:, :3 * chunk, :], S_BT)
        sent(rsb.at[:, :7], S_RS)
        sent(rsb.at[:, :7], S_AG)
        sent(xrecv, S_OC)
        sent(yrecv, S_OY)

    at(999, 999, drain)
    assert counter[0] == recv_sems.shape[0]
    for _, _, fn in sorted(steps, key=lambda s: (s[0], s[1])):
        fn()


def shards(activations, gradients, basis_in, basis_out):
    seq, feat = gradients.shape[1:]
    cols = basis_out.shape[1]
    width = basis_in.shape[1]
    half = (cols + 31) // 32 * 32
    chunk = half // 2
    gt = gradients[0].T
    dims = (feat, seq, half, chunk, width)
    return pl.pallas_call(
        functools.partial(kernel, dims),
        out_shape=jax.ShapeDtypeStruct((cols, width), F32),
        in_specs=[pl.BlockSpec(memory_space=pltpu.HBM)] * 4,
        out_specs=pl.BlockSpec(memory_space=pltpu.VMEM),
        scratch_shapes=[
            pltpu.VMEM((feat, cols), BF16),
            pltpu.VMEM((NYL, 2 * half, feat), BF16),
            pltpu.VMEM((feat, seq), BF16),
            pltpu.VMEM((2, NYL, feat, 4 * seq), BF16),
            pltpu.VMEM((NYL, NZ, seq, width), BF16),
            pltpu.VMEM(basis_in.shape, BF16),
            pltpu.VMEM((seq, width), BF16),
            pltpu.VMEM((4, 2 * seq, 2 * width), BF16),
            pltpu.VMEM((4, NZ, chunk, seq), BF16),
            pltpu.VMEM((4, NZ, chunk, seq), BF16),
            pltpu.VMEM((4, NZ * chunk, seq), BF16),
            pltpu.VMEM((2 * half, 2 * width), F32),
            pltpu.VMEM((half, 2 * width), F32),
            pltpu.VMEM((half, width), BF16),
            pltpu.VMEM((half, width), BF16),
            pltpu.SemaphoreType.DMA((10,)),
            pltpu.SemaphoreType.DMA((145,)),
            pltpu.SemaphoreType.DMA((5,)),
        ],
        compiler_params=pltpu.CompilerParams(
            collective_id=0, has_side_effects=True, vmem_limit_bytes=60 * 1024 * 1024
        ),
        name="ekfac",
    )(basis_out, gt, activations[0], basis_in)


def solution(mesh):
    return jax.shard_map(
        shards,
        mesh=mesh,
        in_specs=(P("dp", None, "mp"), P("dp", None, "mp"), P(None, "mp"), P("mp", "dp")),
        out_specs=P("dp", "mp"),
        check_vma=False,
    )
```

time: 102 us -> 90.6 us (0.89)
  Pallas kernels: 97.8 us -> 88.7 us
  local copies, waits for them, and re-layouts: 3.84 us -> 1.74 us
    pallas_call x1, Pallas kernels: 97.8 us -> 88.7 us  [shards(): pl.pallas_call(functools.partial(kernel, dims), out_shape=jax.ShapeDtypeS...]
    unnamed x2 -> x1, local copies, waits for them, and re-layouts: 3 us -> 1.74 us
where the time goes in v3:
time: 90.6 us; the launch traced here: 90.5 us
  Pallas kernels  88.7 us (98%)
  local copies, waits for them, and re-layouts  1.74 us (2%)
    pallas_call x1, Pallas kernels, shards(): pl.pallas_call(functools.partial(kernel, dims), out_shape=jax.ShapeDtypeS...  88.7 us

profile of v3, /device:TPU:1, one launch (start us, length us, event | category | flops | bytes accessed | tf_op | source)
XLA Modules:
  0.0 90.5 jit_solution(7365122818397766095)
XLA Ops:
  0.0 88.7 %ekfac.1 = f32[344,256]{1,0:T(8,128)} custom-call(bf16[688,344]{1,0:T(8,128)(2,1)} %basis_hbm.1, bf16[688,128]{1,0:T(8,128)(2,1)} %bitcast.4, bf16[128,256]{1,0:T(8,128)(2,1)} %bitcast.5, bf16[4096,256]{1,0:T(8,128)(2,1)} %bin_hbm.1), custom_call_target="tpu_custom_call" | custom-call | tf_op jit(solution)/shard_map/ekfac/pallas_call | solution.py:488
  88.7 1.7 %copy.6 = f32[344,256]{1,0:T(8,128)} copy(f32[344,256]{1,0:T(8,128)} %ekfac.1) | data formatting | bytes 704512

commit v4 on v3

--- a/solution.py
+++ b/solution.py
@@ -265,15 +265,13 @@
 
     def project_acts():
         pltpu.make_async_copy(bin_hbm, binv, loc_sems.at[2]).wait()
-        total = jnp.zeros((seq, width), F32)
+        total = None
         for f in range(2):
             low = (yl if f == 0 else 1 - yl) * NZ
-
-            def body(i, total, f=f, low=low):
-                rows = pl.ds(pl.multiple_of((low + i) * width, 128), width)
-                return total + jnp.dot(act[f, i], binv[rows, :], preferred_element_type=F32)
-
-            total = lax.fori_loop(0, NZ, body, total)
+            rows = pl.ds(pl.multiple_of(low * width, 128), NZ * width)
+            wide = jnp.concatenate([act[f, i] for i in range(NZ)], axis=1)
+            t = jnp.dot(wide, binv[rows, :], preferred_element_type=F32)
+            total = t if total is None else total + t
         paloc[...] = total.astype(BF16)
 
         if is_inner:
@@ -319,30 +317,67 @@
                 s = s_rs + grp * 8 + rs_slot(d, k)
                 send(src, rsb.at[grp, rs_slot(d, k)], S_RS, s, zn[d])
 
+    def rs_two_first(grp):
+        for d in (1, -1):
+            for dist, hop, slot in ((4, 2, 2), (3, 1, 1), (1, 1, 0)):
+                if dist <= rlen(grp, d):
+                    slot = rs_slot(d, slot)
+                    send(part.at[grp, (z + NZ + d * dist) % NZ], rsb.at[grp, slot], S_RS, s_rs + grp * 8 + slot, zn[d * hop])
+
+    def rs_two_middle(grp):
+        for d in (1, -1):
+            total = part[grp, (z + NZ + 2 * d) % NZ].astype(F32)
+            for k in range(1, rlen(grp, d) - 1):
+                slot = rs_slot(d, k)
+                arrived(rsb.at[grp, slot], s_rs + grp * 8 + slot)
+                total = total + rsb[grp, slot].astype(F32)
+            rsb[grp, rs_slot(d, 1)] = total.astype(BF16)
+            slot = rs_slot(d, 3)
+            send(rsb.at[grp, rs_slot(d, 1)], rsb.at[grp, slot], S_RS, s_rs + grp * 8 + slot, zn[2 * d])
+
     def pg_place(grp, j):
         return pg.at[grp, pl.ds(pl.multiple_of(j * chunk, 16), chunk), :]
 
     def ag_sem(grp, d, k):
         return s_ag + grp * 8 + rs_slot(d, k)
 
-    def rs_last(grp):
+    def rs_last(grp, two_steps=False, ag_two_steps=False):
         total = part[grp, z].astype(F32)
         for d in (1, -1):
-            slot = rs_slot(d, rlen(grp, d) - 1)
-            arrived(rsb.at[grp, slot], s_rs + grp * 8 + slot)
-            total = total + rsb[grp, slot].astype(F32)
+            for k in (0, 3) if two_steps else (rlen(grp, d) - 1,):
+                slot = rs_slot(d, k)
+                arrived(rsb.at[grp, slot], s_rs + grp * 8 + slot)
+                total = total + rsb[grp, slot].astype(F32)
         pg[grp, pl.ds(pl.multiple_of(z * chunk, 16), chunk), :] = total.astype(BF16)
-        for d in (1, -1):
-            send(pg_place(grp, z), pg_place(grp, z), S_AG, ag_sem(grp, d, 0), zn[d])
+        for dist in (2, 1) if ag_two_steps else (1,):
+            for d in (1, -1):
+                send(pg_place(grp, z), pg_place(grp, z), S_AG, ag_sem(grp, d, dist - 1), zn[d * dist])
+
+    def ag_wait(grp, d, dist):
+        j = (z + NZ - d * dist) % NZ
+        arrived(pg_place(grp, j), ag_sem(grp, d, dist - 1))
+        return pg_place(grp, j)
 
     def ag_step(grp, k):
         for d in (1, -1):
             n = rlen(grp, d)
             if k <= n:
-                j = (z + NZ - d * k) % NZ
-                arrived(pg_place(grp, j), ag_sem(grp, d, k - 1))
+                piece = ag_wait(grp, d, k)
                 if k < n:
-                    send(pg_place(grp, j), pg_place(grp, j), S_AG, ag_sem(grp, d, k), zn[d])
+                    send(piece, piece, S_AG, ag_sem(grp, d, k), zn[d])
+
+    def ag_two_middle(grp):
+        for d in (1, -1):
+            piece = ag_wait(grp, d, 2)
+            if rlen(grp, d) == 4:
+                send(piece, piece, S_AG, ag_sem(grp, d, 3), zn[2 * d])
+            send(piece, piece, S_AG, ag_sem(grp, d, 2), zn[d])
+
+    def ag_two_last(grp):
+        for dist in (1, 3, 4):
+            for d in (1, -1):
+                if dist <= rlen(grp, d):
+                    ag_wait(grp, d, dist)
 
     def squares(grp, lo, hi):
         a, i = grp // 2, grp % 2
@@ -373,6 +408,9 @@
         arrived(xrecv.at[rows, spans[1]], s_out + 2 * i + 1)
         ysend[rows, :] = (acc[acc_rows(core, i), spans[1]] + xrecv[rows, spans[1]]).astype(BF16)
         send(ysend.at[rows, :], yrecv.at[rows, :], S_OY, s_out + 4 + i, ypart)
+
+    def out_y_of(i, c):
+        pl.when(core == c)(lambda: out_y(i))
 
     def out_last(i):
         rows = slice(i * chunk, (i + 1) * chunk)
@@ -407,50 +445,62 @@
     at(15.5, 18.2, bt_forward, 0)
     at(28, 22.42, x_far, gpat, 0, 0)
     at(28, 22.42, x_far, gpat, 0, 1)
-    at(15.4, 20.5, x_near, gpat, 1, 1)
+    at(15.4, 18.8, x_near, gpat, 1, 1)
     at(20.9, 18.5, x_near, gpat, 1, 0)
     at(18.5, 18.6, bt_ready, 0)
     at(18.6, 18.6, project, 0)
-    at(18.6, 18.6, rs_step, 0, 0)
-    at(21, 19, act_rest)
-    at(21, 19, project_acts)
-    at(21, 19, pa_start)
-    at(22, 22.2, bt_forward, 1)
+    at(18.6, 18.6, rs_two_first, 0)
+    at(20.96, 19, rs_two_middle, 0)
+    at(28.3, 28.3, rs_last, 0, True)
+    for k in range(1, 5):
+        at(28.9 + 3.9 * k, 28.9 + 3.9 * k, ag_step, 0, k)
+    at(25.1, 22.41, act_rest)
+    at(25.1, 22.41, project_acts)
+    at(25.1, 22.41, pa_start)
+    at(20.95, 18.7, bt_forward, 1)
     at(25, 22.4, bt_ready, 1)
     at(25, 22.4, project, 1)
     at(25, 22.4, rs_step, 1, 0)
     at(28, 28, x_far, gpat, 1, 0)
     at(28, 28, x_far, gpat, 1, 1)
     for grp in (2, 3):
-        at(28, 28, project, grp)
-        at(28, 28, rs_step, grp, 0)
-    at(22, 28.62, y_near_own, ppat)
-    at(32.5, 28.61, y_near_other, ppat, None)
-    at(41.1, 28.63, y_far_own, ppat)
+        at(28 + grp / 20, 28 + grp / 20, project, grp)
+        at(28 + grp / 20, 28 + grp / 20, rs_step, grp, 0)
+    at(25.2, 33.46, y_near_own, ppat)
+    at(33.45, 33.45, y_near_other, ppat, None)
+    at(41.1, 33.47, y_far_own, ppat)
     at(41, 41, y_far_other, ppat, None)
     for i, (a, f) in enumerate(((0, 0), (0, 1), (1, 1), (1, 0))):
         t = (43, 43, 47.4, 47.4)[i]
         at(t, t, x_near, ppat, a, f)
         t = (48, 48, 54.8, 54.8)[i]
         at(t, t, x_far, ppat, a, f)
-    for grp, r0, a0 in ((0, 23, 34), (1, 29, 40.2), (2, 32, 43.3), (3, 32.1, 43.4)):
-        for k in (1, 2, 3):
-            t = r0 + 3.7 * (k - 1) + (2 if grp == 0 and k > 1 and not is_inner else 0)
-            at(t, t, rs_step, grp, k)
-        at(a0, a0, rs_last, grp)
-        for k in (1, 2, 3, 4):
-            t = a0 + 3.7 * k
-            at(t, t, ag_step, grp, k)
-    at(50, 50, squares, 0, 0, 2 * width)
-    at(56, 56, squares, 1, 0, 2 * width)
-    at(58.15, 58.15, squares, 2, 0, 2 * width)
-    at(58.15, 58.15, out_core, 0, 1)
-    at(58.15, 58.15, out_core, 0, 0)
+    for grp, t_in, t_out, t_last in (
+        (1, (28.25, 33.5, 37.5), (28.25, 33.5, 37.5), 41),
+        (2, (32, 33.4, 37.4), (32, 33.4, 37.4), 40.9),
+        (3, (32.1, 34, 38), (32.1, 34, 38), 41.5),
+    ):
+        for k in range(3):
+            at(t_in[k], t_out[k], rs_step, grp, k + 1)
+        two = grp in ()
+        at(t_last, t_last, rs_last, grp, False, two)
+        if two:
+            at(t_last + 4.9, t_last + 4.9, ag_two_middle, grp)
+            at(t_last + 9.9, t_last + 9.9, ag_two_last, grp)
+        else:
+            for k in range(1, 5):
+                at(t_last + 4 * k, t_last + 4 * k, ag_step, grp, k)
+    at(53, 53, squares, 0, 0, 2 * width)
+    at(56.95, 56.95, squares, 2, 0, 2 * width)
+    at(56.95, 56.95, out_core, 0, 1)
+    at(56.95, 56.95, out_core, 0, 0)
+    at(57.1, 57.1, squares, 1, 0, 2 * width)
+    at(57.05, 57.05, out_y_of, 0, 0)
+    at(59.15, 59.15, out_y_of, 0, 1)
     at(59, 59, squares, 3, width, 2 * width)
     at(59, 59, out_core, 1, 1)
     at(59.1, 59.1, squares, 3, 0, width)
     at(59.2, 59.2, out_core, 1, 0)
-    at(59.3, 59.3, out_y, 0)
     at(61, 61, out_y, 1)
     at(62, 62, out_last, 0)
     at(63, 63, out_last, 1)
@@ -511,10 +561,10 @@
             pltpu.SemaphoreType.DMA((5,)),
         ],
         compiler_params=pltpu.CompilerParams(
-            collective_id=0, has_side_effects=True, vmem_limit_bytes=60 * 1024 * 1024
+            collective_id=0, has_side_effects=True, vmem_limit_bytes=40 * 1024 * 1024
         ),
         name="ekfac",
-    )(basis_out, gt, activations[0], basis_in)
+    )(*[pltpu.with_memory_space_constraint(v, pltpu.HBM) for v in (basis_out, gt, activations[0], basis_in)])
 
 
 def solution(mesh):

time: 90.6 us -> 85 us (0.938)
  Pallas kernels: 88.7 us -> 84.1 us
  local copies, waits for them, and re-layouts: 1.74 us -> 0.74 us
    pallas_call x1, Pallas kernels: 88.7 us -> 84.1 us  [shards(): pl.pallas_call(functools.partial(kernel, dims), out_shape=jax.ShapeDtypeS...]
    unnamed x1, local copies, waits for them, and re-layouts: 1.74 us -> 0.74 us
where the time goes in v4:
time: 85 us; the launch traced here: 84.9 us
  Pallas kernels  84.1 us (99%)
    pallas_call x1, Pallas kernels, shards(): pl.pallas_call(functools.partial(kernel, dims), out_shape=jax.ShapeDtypeS...  84.1 us

profile of v4, /device:TPU:1, one launch (start us, length us, event | category | flops | bytes accessed | tf_op | source)
XLA Modules:
  0.0 84.9 jit_solution(4811403429423057786)
XLA Ops:
  0.0 84.1 %ekfac.1 = f32[344,256]{1,0:T(8,128)S(1)} custom-call(bf16[688,344]{1,0:T(8,128)(2,1)} %basis_hbm.1, bf16[688,128]{1,0:T(8,128)(2,1)} %bitcast.4, bf16[128,256]{1,0:T(8,128)(2,1)} %bitcast.5, bf16[4096,256]{1,0:T(8,128)(2,1)} %bin_hbm.1), custom_call_target="tpu_custom_call" | custom-call | tf_op jit(solution)/shard_map/ekfac/pallas_call | solution.py:538
  84.1 0.7 copy.6

commit v5 on v4

--- a/solution.py
+++ b/solution.py
@@ -379,7 +379,7 @@
                 if dist <= rlen(grp, d):
                     ag_wait(grp, d, dist)
 
-    def squares(grp, lo, hi):
+    def squares(grp, lo, hi, whose=None):
         a, i = grp // 2, grp % 2
 
         def body(c, carry):
@@ -392,7 +392,10 @@
             acc[rows, lo:hi] = total
             return carry
 
-        lax.fori_loop(0, 2, body, 0)
+        if whose is None:
+            lax.fori_loop(0, 2, body, 0)
+        else:
+            body(core if whose else 1 - core, 0)
 
     spans = (slice(0, width), slice(width, 2 * width))
 
@@ -496,11 +499,13 @@
     at(56.95, 56.95, out_core, 0, 0)
     at(57.1, 57.1, squares, 1, 0, 2 * width)
     at(57.05, 57.05, out_y_of, 0, 0)
-    at(59.15, 59.15, out_y_of, 0, 1)
-    at(59, 59, squares, 3, width, 2 * width)
+    at(59, 59, squares, 3, width, 2 * width, 0)
     at(59, 59, out_core, 1, 1)
-    at(59.1, 59.1, squares, 3, 0, width)
-    at(59.2, 59.2, out_core, 1, 0)
+    at(59, 59, squares, 3, 0, width, 0)
+    at(59, 59, out_core, 1, 0)
+    at(59, 59, squares, 3, width, 2 * width, 1)
+    at(59, 59, out_y_of, 0, 1)
+    at(61.1, 61.1, squares, 3, 0, width, 1)
     at(61, 61, out_y, 1)
     at(62, 62, out_last, 0)
     at(63, 63, out_last, 1)

time: 85 us -> 84.9 us (level)
  no operation moved by 1% of the time
where the time goes in v5:
time: 84.9 us; the launch traced here: 84.8 us
  Pallas kernels  84.1 us (99%)
    pallas_call x1, Pallas kernels, shards(): pl.pallas_call(functools.partial(kernel, dims), out_shape=jax.ShapeDtypeS...  84.1 us

profile of v5, /device:TPU:1, one launch (start us, length us, event | category | flops | bytes accessed | tf_op | source)
XLA Modules:
  0.0 84.8 jit_solution(14120656982401073860)
XLA Ops:
  0.0 84.1 %ekfac.1 = f32[344,256]{1,0:T(8,128)S(1)} custom-call(bf16[688,344]{1,0:T(8,128)(2,1)} %basis_hbm.1, bf16[688,128]{1,0:T(8,128)(2,1)} %bitcast.4, bf16[128,256]{1,0:T(8,128)(2,1)} %bitcast.5, bf16[4096,256]{1,0:T(8,128)(2,1)} %bin_hbm.1), custom_call_target="tpu_custom_call" | custom-call | tf_op jit(solution)/shard_map/ekfac/pallas_call | solution.py:543
  84.1 0.7 copy.6

commit v6 on v5

--- a/solution.py
+++ b/solution.py
@@ -51,16 +51,15 @@
     def own_block():
         return g.at[0, 0, :, :seq]
 
+    barrier = pltpu.get_barrier_semaphore()
+    peers = [ydev(2), ydev(-2), zn[2], zn[-2], ydev(1), ydev(-1), xn[1], xn[-1], zn[1], zn[-1], sibling]
+    for peer in peers:
+        pl.semaphore_signal(barrier, inc=1, device_id=peer, device_id_type=MESH)
     pltpu.make_async_copy(gt_hbm, gt, loc_sems.at[0]).start()
     pltpu.make_async_copy(act_hbm, act.at[0, z], loc_sems.at[1]).start()
     pltpu.make_async_copy(basis_hbm, raw, loc_sems.at[4]).start()
     pltpu.make_async_copy(bin_hbm, binv, loc_sems.at[2]).start()
     pl.when(inner)(lambda: pltpu.make_async_copy(gt_hbm, own_block(), loc_sems.at[3]).start())
-
-    barrier = pltpu.get_barrier_semaphore()
-    peers = [sibling, xn[1], xn[-1], zn[1], zn[-1], zn[2], zn[-2], ydev(1), ydev(-1), ydev(2), ydev(-2)]
-    for peer in peers:
-        pl.semaphore_signal(barrier, inc=1, device_id=peer, device_id_type=MESH)
     pl.semaphore_wait(barrier, len(peers))
 
     refs = (basis_hbm, gt_hbm, act_hbm, bin_hbm, out_ref, raw, bt, gt, g, act, binv, paloc, pa, part, rsb, pg, acc,

time: 84.9 us -> 84.6 us (level)
  no operation moved by 1% of the time
where the time goes in v6:
time: 84.6 us; the launch traced here: 84.5 us
  Pallas kernels  83.7 us (99%)
    pallas_call x1, Pallas kernels, shards(): pl.pallas_call(functools.partial(kernel, dims), out_shape=jax.ShapeDtypeS...  83.7 us

profile of v6, /device:TPU:1, one launch (start us, length us, event | category | flops | bytes accessed | tf_op | source)
XLA Modules:
  0.0 84.5 jit_solution(2993201292674791845)
XLA Ops:
  0.0 83.7 %ekfac.1 = f32[344,256]{1,0:T(8,128)S(1)} custom-call(bf16[688,344]{1,0:T(8,128)(2,1)} %basis_hbm.1, bf16[688,128]{1,0:T(8,128)(2,1)} %bitcast.4, bf16[128,256]{1,0:T(8,128)(2,1)} %bitcast.5, bf16[4096,256]{1,0:T(8,128)(2,1)} %bin_hbm.1), custom_call_target="tpu_custom_call" | custom-call | tf_op jit(solution)/shard_map/ekfac/pallas_call | solution.py:542
  83.7 0.7 copy.6
